TPU v7x, 32 devices: a whole 2x2x4 slice. The times are simulated.
32 devices in a mesh: head: 8 (over z, core), kv: 4 (over y, x).
Axes of the slice: x: 2, y: 2, z: 4, core: 2. Of those that a mesh axis runs over, the one named last changes fastest.
Arguments:
- queries: bfloat16 [2048, 8192], P(('kv', 'head')), may hold values from -6 to 6
- key_rows: bfloat16 [2048, 1024], P(('kv', 'head')), may hold values from -6 to 6
- value_matrix: bfloat16 [2048, 1024], P(('kv', 'head')), may hold values from -6 to 6
- doc_ids: int32 [2048], P(('kv', 'head')), may hold values from 0 to 5, as said below
Outputs:
- attended: bfloat16 [2048, 8192], P(('kv', 'head'))
Inputs may be any that keep to these rules, and one draw needn't show every extreme that they name: doc_ids starts at 0, never falls, and rises by one at the first token of each of the 6 documents; every document starts at an even position and has 2 tokens or more.
All inputs are finite; a program needn't handle non-finite values.
Results may differ from a plain program's by a relative error of at most 0.015.
Values may be sent and summed in bfloat16 or wider, within the bound.
A program may use at most 64 MiB of HBM per device.

v0:
```python
import math
import jax
import jax.numpy as jnp
from jax import lax
from jax.sharding import PartitionSpec as P

QUERY_HEADS = 64
KEY_VALUE_HEADS = 8
HEAD_SIZE = 128
NEG_FILL = -1e30


def repeat_heads(input_matrix, head_repeats):
    row_number = input_matrix.shape[0]
    heads_apart = input_matrix.reshape(row_number, KEY_VALUE_HEADS, 1, HEAD_SIZE)
    expanded_heads = jnp.broadcast_to(
        heads_apart, (row_number, KEY_VALUE_HEADS, head_repeats, HEAD_SIZE)
    )
    return expanded_heads.reshape(row_number, KEY_VALUE_HEADS * head_repeats * HEAD_SIZE)


def block_terms(query_group, query_pos, query_doc, key_block, value_block, key_pos, key_doc):
    key_count = key_block.shape[0]
    key_value_slot = query_group.shape[1]
    key_heads = key_block.reshape(key_count, key_value_slot, HEAD_SIZE)
    value_heads = value_block.reshape(key_count, key_value_slot, HEAD_SIZE)
    scores = jnp.einsum(
        "rkgd,ckd->kgrc", query_group, key_heads, preferred_element_type=jnp.float32
    ) * HEAD_SIZE ** (-0.5)
    allowed = (key_pos[None, :] <= query_pos[:, None]) & (key_doc[None, :] == query_doc[:, None])
    masked = jnp.where(allowed, scores, NEG_FILL)
    row_peak = jnp.max(masked, axis=-1)
    weights = jnp.where(allowed, jnp.exp(masked - row_peak[..., None]), 0.0)
    row_total = jnp.sum(weights, axis=-1)
    weighted = jnp.einsum(
        "kgrc,ckd->kgrd",
        weights.astype(jnp.bfloat16),
        value_heads,
        preferred_element_type=jnp.float32,
    )
    return (row_peak, row_total, weighted)


def attend_block(query_group, query_pos, query_doc, key_block, value_block, key_pos, key_doc):
    return block_terms(query_group, query_pos, query_doc, key_block, value_block, key_pos, key_doc)


def combine_terms(first_terms, second_terms):
    joint_peak = jnp.maximum(first_terms[0], second_terms[0])
    left_factor = jnp.exp(first_terms[0] - joint_peak)
    right_factor = jnp.exp(second_terms[0] - joint_peak)
    joint_total = first_terms[1] * left_factor + second_terms[1] * right_factor
    joint_weighted = (
        first_terms[2] * left_factor[..., None] + second_terms[2] * right_factor[..., None]
    )
    return (joint_peak, joint_total, joint_weighted)


def local(queries, key_rows, value_matrix, doc_ids):
    head_number = lax.axis_size("head")
    head_repeats = max(1, head_number // KEY_VALUE_HEADS)
    key_send = repeat_heads(key_rows, head_repeats)
    value_send = repeat_heads(value_matrix, head_repeats)
    query_block, key_block, value_block = (
        lax.all_to_all(queries, "head", split_axis=1, concat_axis=0, tiled=True),
        lax.all_to_all(key_send, "head", split_axis=1, concat_axis=0, tiled=True),
        lax.all_to_all(value_send, "head", split_axis=1, concat_axis=0, tiled=True),
    )
    block_len = query_block.shape[0]
    doc_global = lax.all_gather(doc_ids, ("kv", "head"), axis=0, tiled=True)
    query_width = query_block.shape[1]
    present_heads = query_width // HEAD_SIZE
    key_value_slot = max(1, present_heads // (QUERY_HEADS // KEY_VALUE_HEADS))
    group_here = present_heads // key_value_slot
    own_first = lax.axis_index("kv") * block_len
    own_pos = own_first + jnp.arange(block_len, dtype=jnp.int32)
    own_doc = jnp.take(doc_global, own_pos)
    query_group = query_block.reshape(block_len, key_value_slot, group_here, HEAD_SIZE)
    term_shape = (key_value_slot, group_here, block_len)
    initial = (
        jnp.full(term_shape, NEG_FILL, jnp.float32),
        jnp.zeros(term_shape, jnp.float32),
        jnp.zeros(term_shape + (HEAD_SIZE,), jnp.float32),
    )
    key_piece = lax.all_gather(key_block, "kv", axis=0, tiled=True)
    value_piece = lax.all_gather(value_block, "kv", axis=0, tiled=True)
    piece_rows = key_piece.shape[0]
    step_rows = math.gcd(piece_rows, 1024)

    def one_step(step_index, inner):
        local_first = step_index * step_rows
        keys_now = lax.dynamic_slice_in_dim(key_piece, local_first, step_rows, 0)
        values_now = lax.dynamic_slice_in_dim(value_piece, local_first, step_rows, 0)
        key_pos = local_first + jnp.arange(step_rows, dtype=jnp.int32)
        key_doc = jnp.take(doc_global, key_pos)
        return combine_terms(
            inner,
            attend_block(query_group, own_pos, own_doc, keys_now, values_now, key_pos, key_doc),
        )

    folded = lax.fori_loop(0, piece_rows // step_rows, one_step, initial)
    result = (
        (folded[2] / folded[1][..., None]).transpose(2, 0, 1, 3).reshape(block_len, query_width)
    )
    result = result.astype(jnp.bfloat16)
    return lax.all_to_all(result, "head", split_axis=0, concat_axis=1, tiled=True)


def solution(mesh):
    return jax.shard_map(
        local,
        mesh=mesh,
        in_specs=(
            P(("kv", "head"), None),
            P(("kv", "head"), None),
            P(("kv", "head"), None),
            P(("kv", "head")),
        ),
        out_specs=P(("kv", "head"), None),
        check_vma=False,
    )
```

profile of v0, /device:TPU:0, one launch (start us, length us, event | category | flops | bytes accessed | tf_op | source)
XLA Modules:
  0.0 176.7 jit_solution(10033229204570758715)
XLA Ops:
  0.0 0.0 copy-start
  0.0 0.9 copy-done
  0.9 0.7 copy_bitcast_fusion.2
  1.6 6.4 %all-to-all-start = ((bf16[64,8,128]{2,0,1:T(8,128)(2,1)}), bf16[64,8,128]{2,0,1:T(8,128)(2,1)S(1)}, u32[]{:S(2)}, u32[]{:S(2)}) async-start(bf16[64,8,128]{2,0,1:T(8,128)(2,1)} %copy_bitcast_fusion.2), calls=%async_computation | async-start | bytes 262144 | tf_op jit(solution)/shard_map/all_to_all | solution.py:66
  7.9 1.6 copy_bitcast_fusion.1
  9.5 5.2 %all-to-all-done = bf16[64,8,128]{2,0,1:T(8,128)(2,1)S(1)} async-done(((bf16[64,8,128]{2,0,1:T(8,128)(2,1)}), bf16[64,8,128]{2,0,1:T(8,128)(2,1)S(1)}, u32[]{:S(2)}, u32[]{:S(2)}) %all-to-all-start) | async-done | bytes 131104 | tf_op jit(solution)/shard_map/all_to_all | solution.py:66
  14.7 3.4 %all-to-all-start.2 = ((bf16[64,8,128]{2,0,1:T(8,128)(2,1)}), bf16[64,8,128]{2,0,1:T(8,128)(2,1)S(1)}, u32[]{:S(2)}, u32[]{:S(2)}) async-start(bf16[64,8,128]{2,0,1:T(8,128)(2,1)} %copy_bitcast_fusion.1), calls=%async_computation.2 | async-start | bytes 262144 | tf_op jit(solution)/shard_map/all_to_all | solution.py:67
  18.1 2.3 %copy.30 = bf16[8,8,8,1024]{3,2,0,1:T(8,128)(2,1)} copy(bf16[8,8,8,1024]{3,2,1,0:T(8,128)(2,1)} %bitcast.121) | data formatting | bytes 2097152 | tf_op jit(solution)/shard_map/all_to_all | solution.py:65
  20.4 4.4 %all-to-all-done.2 = bf16[64,8,128]{2,0,1:T(8,128)(2,1)S(1)} async-done(((bf16[64,8,128]{2,0,1:T(8,128)(2,1)}), bf16[64,8,128]{2,0,1:T(8,128)(2,1)S(1)}, u32[]{:S(2)}, u32[]{:S(2)}) %all-to-all-start.2) | async-done | bytes 131104 | tf_op jit(solution)/shard_map/all_to_all | solution.py:67
  24.8 3.6 %all-to-all-start.1 = ((bf16[64,8,1024]{2,0,1:T(8,128)(2,1)}), bf16[64,8,1024]{2,0,1:T(8,128)(2,1)S(1)}, u32[]{:S(2)}, u32[]{:S(2)}) async-start(bf16[64,8,1024]{2,0,1:T(8,128)(2,1)} %bitcast.93), calls=%async_computation.1 | async-start | bytes 2097152 | tf_op jit(solution)/shard_map/all_to_all | solution.py:65
  28.4 1.3 dynamic-slice
  30.4 0.9 dynamic-update-slice
  31.2 43.9 %all-reduce = s32[2048]{0:T(1024)S(1)} all-reduce(s32[2048]{0:T(1024)S(1)} %dynamic-update-slice), channel_id=1, replica_groups=mesh['head'=8,'kv'=4] {'kv','head'}, use_global_device_ids=true, to_apply=%add | all-reduce | flops 2048 | bytes 16384
  75.2 3.1 %gather_fusion.1 = s32[512]{0:T(512)S(1)} fusion(s32[2048]{0:T(1024)S(1)} %all-reduce, s32[1024]{0:T(1024)S(1)} %pad_clamp_fusion), kind=kCustom, calls=%fused_computation.1 | custom fusion | bytes 6144 | tf_op jit(solution)/shard_map/jit(_take)/gather | solution.py:77
  78.3 11.6 %all_gather.11 = bf16[2048,128]{1,0:T(8,128)(2,1)S(1)} all-gather(bf16[512,128]{1,0:T(8,128)(2,1)S(1)} %bitcast.124), channel_id=1, replica_groups=mesh['head'=8,'kv'=4] {'kv'}, dimensions={0}, use_global_device_ids=true | all-gather | bytes 655360 | tf_op jit(solution)/shard_map/all_gather | solution.py:86
  89.9 9.0 %all_gather.10 = bf16[2048,128]{1,0:T(8,128)(2,1)S(1)} all-gather(bf16[512,128]{1,0:T(8,128)(2,1)S(1)} %bitcast.123), channel_id=1, replica_groups=mesh['head'=8,'kv'=4] {'kv'}, dimensions={0}, use_global_device_ids=true | all-gather | bytes 655360 | tf_op jit(solution)/shard_map/all_gather | solution.py:85
  98.9 0.0 all-to-all-done.1
  98.9 0.3 copy.26
  99.2 0.1 copy.18
  99.3 43.2 %while.18 = (s32[]{:T(128)}, f32[1,8,512]{2,1,0:T(8,128)S(1)}, f32[1,8,512]{2,1,0:T(8,128)S(1)}, f32[1,8,512,128]{3,2,1,0:T(8,128)}, s32[2048]{0:T(1024)S(1)}, /...) while((s32[]{:T(128)}, f32[1,8,512]{2,1,0:T(8,128)S(1)}, ...), condition=%wide.region_3.4_spmd.clone, body=%wide.region_0.3_spmd.clone.sunk | while | flops 2205726208 | bytes 75335952 | solution.py:101
  99.4 6.2 %gather_fusion = s32[1024]{0:T(1024)S(1)} fusion(s32[2048]{0:T(1024)S(1)} %get-tuple-element.370, s32[1024]{0:T(1024)S(1)} %broadcast_clamp_fusion.2), kind=kCustom, calls=%fused_computation.clone.clone.1 | custom fusion | bytes 12288 | tf_op jit(solution)/shard_map/while/body/eval_jaxpr/jit(_take)/gather | solution.py:95
  105.6 0.8 compare_and_fusion.2
  106.4 2.9 %fusion.41 = (f32[8,512]{1,0:T(8,128)S(1)}, f32[1024,512,8]{1,0,2:T(8,128)S(1)}) fusion(pred[512,1024]{0,1:T(8,128)(4,1)S(1)} %compare_and_fusion.2, bf16[512,1,8,128]{3,0,2,1:T(8,128)(2,1)S(1)} %get-tuple-element.373, bf16[2048,128]{1,0:T(8,128)(2,1)S(1)} %get-tuple-element.372, s32[]{:T(128)S(6)} %select_n.145), kind=kOutput, calls=%fused_computation.5.clone.1 | convolution fusion | flops 1086320640 | bytes 18628612 | tf_op jit(solution)/shard_map/while/body/eval_jaxpr/rkgd,ckd->kgrc/dot_general | solution.py:27
  109.3 0.0 copy-start.1
  109.3 4.0 %fusion.43 = f32[8,512]{1,0:T(8,128)S(1)} fusion(f32[1024,512,8]{1,0,2:T(8,128)S(1)} %get-tuple-element.334, f32[8,512]{1,0:T(8,128)S(1)} %get-tuple-element.332, pred[512,1024]{0,1:T(8,128)(4,1)S(1)} %compare_and_fusion.2), kind=kLoop, calls=%fused_computation.7.clone.1 | loop fusion | flops 20967424 | bytes 17334272 | tf_op jit(solution)/shard_map/while/body/eval_jaxpr/reduce_sum | solution.py:34
  113.4 0.0 copy-done.1
  113.4 6.1 %bitcast_add_fusion.2 = f32[1,8,512,128]{3,2,1,0:T(8,128)S(1)} fusion(f32[1,8,512,128]{3,2,1,0:T(8,128)S(1)} %copy-done.1, f32[1024,512,8]{1,0,2:T(8,128)S(1)} %get-tuple-element.334, f32[8,512]{1,0:T(8,128)S(1)} %get-tuple-element.332, pred[512,1024]{0,1:T(8,128)(4,1)S(1)} %compare_and_fusion.2, f32[8,512]{1,0:T(8,128)S(1)} %get-tuple-element.336, ...), kind=kOutput, calls=%fused_computation.11.clone.1 | convolution fusion | flops 1096810496 | bytes 21807108 | tf_op jit(solution)/shard_map/while/body/eval_jaxpr/kgrc,ckd->kgrd/dot_general | solution.py:35
  119.6 0.0 copy-start.2
  119.6 1.3 copy-done.2
  120.9 6.2 %gather_fusion = s32[1024]{0:T(1024)S(1)} fusion(s32[2048]{0:T(1024)S(1)} %get-tuple-element.370, s32[1024]{0:T(1024)S(1)} %broadcast_clamp_fusion.2), kind=kCustom, calls=%fused_computation.clone.clone.1 | custom fusion | bytes 12288 | tf_op jit(solution)/shard_map/while/body/eval_jaxpr/jit(_take)/gather | solution.py:95
  127.1 0.8 compare_and_fusion.2
  128.0 2.9 %fusion.41 = (f32[8,512]{1,0:T(8,128)S(1)}, f32[1024,512,8]{1,0,2:T(8,128)S(1)}) fusion(pred[512,1024]{0,1:T(8,128)(4,1)S(1)} %compare_and_fusion.2, bf16[512,1,8,128]{3,0,2,1:T(8,128)(2,1)S(1)} %get-tuple-element.373, bf16[2048,128]{1,0:T(8,128)(2,1)S(1)} %get-tuple-element.372, s32[]{:T(128)S(6)} %select_n.145), kind=kOutput, calls=%fused_computation.5.clone.1 | convolution fusion | flops 1086320640 | bytes 18628612 | tf_op jit(solution)/shard_map/while/body/eval_jaxpr/rkgd,ckd->kgrc/dot_general | solution.py:27
  130.9 0.0 copy-start.1
  130.9 4.0 %fusion.43 = f32[8,512]{1,0:T(8,128)S(1)} fusion(f32[1024,512,8]{1,0,2:T(8,128)S(1)} %get-tuple-element.334, f32[8,512]{1,0:T(8,128)S(1)} %get-tuple-element.332, pred[512,1024]{0,1:T(8,128)(4,1)S(1)} %compare_and_fusion.2), kind=kLoop, calls=%fused_computation.7.clone.1 | loop fusion | flops 20967424 | bytes 17334272 | tf_op jit(solution)/shard_map/while/body/eval_jaxpr/reduce_sum | solution.py:34
  135.0 0.0 copy-done.1
  135.0 6.1 %bitcast_add_fusion.2 = f32[1,8,512,128]{3,2,1,0:T(8,128)S(1)} fusion(f32[1,8,512,128]{3,2,1,0:T(8,128)S(1)} %copy-done.1, f32[1024,512,8]{1,0,2:T(8,128)S(1)} %get-tuple-element.334, f32[8,512]{1,0:T(8,128)S(1)} %get-tuple-element.332, pred[512,1024]{0,1:T(8,128)(4,1)S(1)} %compare_and_fusion.2, f32[8,512]{1,0:T(8,128)S(1)} %get-tuple-element.336, ...), kind=kOutput, calls=%fused_computation.11.clone.1 | convolution fusion | flops 1096810496 | bytes 21807108 | tf_op jit(solution)/shard_map/while/body/eval_jaxpr/kgrc,ckd->kgrd/dot_general | solution.py:35
  141.1 0.0 copy-start.2
  141.2 1.3 copy-done.2
  142.5 2.0 %fusion.26 = bf16[512,1,8,128]{3,0,2,1:T(8,128)(2,1)S(1)} fusion(f32[1,8,512,128]{3,2,1,0:T(8,128)} %get-tuple-element.175, f32[8,512]{1,0:T(8,128)S(1)} %bitcast.122), kind=kLoop, calls=%fused_computation.42 | loop fusion | flops 1048576 | bytes 3162112 | tf_op jit(solution)/shard_map/convert_element_type | solution.py:105
  144.4 0.7 copy.19
  145.1 0.5 convert_element_type.19
  145.6 30.0 %all_to_all.70 = bf16[8,64,1024]{2,1,0:T(8,128)(2,1)S(1)} all-to-all(bf16[8,64,1024]{2,1,0:T(8,128)(2,1)S(1)} %convert_element_type.19), channel_id=1, replica_groups=mesh['head'=8,'kv'=4] {'head'}, dimensions={0} | all-to-all | bytes 2097152 | tf_op jit(solution)/shard_map/all_to_all | solution.py:106
  175.6 1.1 copy.25
  (21 shorter events, 0.2 us)
Async XLA Ops:
  0.0 0.9 copy-start
  1.6 13.1 %all-to-all-start = ((bf16[64,8,128]{2,0,1:T(8,128)(2,1)}), bf16[64,8,128]{2,0,1:T(8,128)(2,1)S(1)}, u32[]{:S(2)}, u32[]{:S(2)}) async-start(bf16[64,8,128]{2,0,1:T(8,128)(2,1)} %copy_bitcast_fusion.2), calls=%async_computation | async-start | bytes 262144 | tf_op jit(solution)/shard_map/all_to_all | solution.py:66
  14.7 10.1 %all-to-all-start.2 = ((bf16[64,8,128]{2,0,1:T(8,128)(2,1)}), bf16[64,8,128]{2,0,1:T(8,128)(2,1)S(1)}, u32[]{:S(2)}, u32[]{:S(2)}) async-start(bf16[64,8,128]{2,0,1:T(8,128)(2,1)} %copy_bitcast_fusion.1), calls=%async_computation.2 | async-start | bytes 262144 | tf_op jit(solution)/shard_map/all_to_all | solution.py:67
  24.8 74.1 %all-to-all-start.1 = ((bf16[64,8,1024]{2,0,1:T(8,128)(2,1)}), bf16[64,8,1024]{2,0,1:T(8,128)(2,1)S(1)}, u32[]{:S(2)}, u32[]{:S(2)}) async-start(bf16[64,8,1024]{2,0,1:T(8,128)(2,1)} %bitcast.93), calls=%async_computation.1 | async-start | bytes 2097152 | tf_op jit(solution)/shard_map/all_to_all | solution.py:65
  109.3 4.1 %copy-start.1 = (f32[1,8,512,128]{3,2,1,0:T(8,128)S(1)}, f32[1,8,512,128]{3,2,1,0:T(8,128)}, u32[]{:S(2)}) copy-start(f32[1,8,512,128]{3,2,1,0:T(8,128)} %get-tuple-element.355) | copy-start | bytes 6291460 | tf_op jit(solution)/shard_map/while
  119.6 1.3 copy-start.2
  130.9 4.1 %copy-start.1 = (f32[1,8,512,128]{3,2,1,0:T(8,128)S(1)}, f32[1,8,512,128]{3,2,1,0:T(8,128)}, u32[]{:S(2)}) copy-start(f32[1,8,512,128]{3,2,1,0:T(8,128)} %get-tuple-element.355) | copy-start | bytes 6291460 | tf_op jit(solution)/shard_map/while
  141.1 1.3 copy-start.2
where the time goes:
time: 177 us
  blocking collectives  94.4 us (53%)
  local copies, waits for them, and re-layouts  28.4 us (16%)
  matrix products  18.1 us (10%)
  starting transfers between devices  13.3 us (8%)
  other arithmetic  11.8 us (7%)
  waiting for transfers between devices  9.58 us (5%)
    unnamed x1, blocking collectives  43.9 us
    all_to_all x1, blocking collectives, local(): lax.all_to_all(result, 'head', split_axis=0, concat_axis=1, tiled=True)  30 us
    gather x2, local copies, waits for them, and re-layouts, one_step(): key_doc = jnp.take(doc_global, key_pos)  12.3 us
    dot_general x2, matrix products, block_terms(): jnp.einsum('kgrc,ckd->kgrd', weights.astype(jnp.bfloat16), value_heads, p...  12.3 us
    all_gather x1, blocking collectives, local(): value_piece = lax.all_gather(value_block, 'kv', axis=0, tiled=True)  11.6 us
    all_gather x1, blocking collectives, local(): key_piece = lax.all_gather(key_block, 'kv', axis=0, tiled=True)  9 us
    reduce_sum x2, other arithmetic, block_terms(): row_total = jnp.sum(weights, axis=-1)  8.05 us
    all_to_all x1, starting transfers between devices, local(): lax.all_to_all(key_send, 'head', split_axis=1, concat_axis=0, tiled=True)  6.35 us
  transfers between devices with their start and end apart: 3, of which 2 were waited for; matrix products, arithmetic and copies ran while one was open for 5% of the time, Pallas kernels for 0%

commit v1 on v0

--- a/solution.py
+++ b/solution.py
@@ -8,6 +8,16 @@
 KEY_VALUE_HEADS = 8
 HEAD_SIZE = 128
 NEG_FILL = -1e30
+
+
+def pass_along(value, mesh_axis, d):
+    size = lax.axis_size(mesh_axis)
+    held, pieces = (value, [value])
+    for _ in range(size - 1):
+        held = lax.ppermute(held, mesh_axis, [(i, (i + 1) % size) for i in range(size)])
+        pieces.insert(0, held)
+    line = jnp.concatenate(pieces, axis=d)
+    return jnp.roll(line, (lax.axis_index(mesh_axis) + 1) * value.shape[d], axis=d)
 
 
 def repeat_heads(input_matrix, head_repeats):
@@ -82,7 +92,7 @@
         jnp.zeros(term_shape, jnp.float32),
         jnp.zeros(term_shape + (HEAD_SIZE,), jnp.float32),
     )
-    key_piece = lax.all_gather(key_block, "kv", axis=0, tiled=True)
+    key_piece = pass_along(key_block, "kv", 0)
     value_piece = lax.all_gather(value_block, "kv", axis=0, tiled=True)
     piece_rows = key_piece.shape[0]
     step_rows = math.gcd(piece_rows, 1024)

time: 177 us -> 170 us (0.960)
  blocking collectives: 94.4 us -> 83 us
  starting transfers between devices: 13.3 us -> 18.7 us
    all_gather x1 -> x0, blocking collectives: 9 us -> none  [local(): key_piece = lax.all_gather(key_block, 'kv', axis=0, tiled=True)]
    ppermute x0 -> x3, starting transfers between devices: none -> 5.41 us  [pass_along(): lax.ppermute(held, mesh_axis, [(i, (i + 1) % size) for i in range(size)])]
    unnamed x7 -> x14, local copies, waits for them, and re-layouts: 3.49 us -> 3.62 us
  transfers between devices with their start and end apart: 3 -> 6, of which waited for: 2 -> 2; matrix products, arithmetic and copies ran while one was open for 5% -> 6% of each run, Pallas kernels for 0% -> 0%
where the time goes in v1:
time: 170 us
  blocking collectives  83 us (49%)
  local copies, waits for them, and re-layouts  28.6 us (17%)
  starting transfers between devices  18.7 us (11%)
  matrix products  18.3 us (11%)
  other arithmetic  11.8 us (7%)
  waiting for transfers between devices  8.04 us (5%)
    unnamed x1, blocking collectives  42.4 us
    all_to_all x1, blocking collectives, local(): lax.all_to_all(result, 'head', split_axis=0, concat_axis=1, tiled=True)  30 us
    dot_general x2, matrix products, block_terms(): jnp.einsum('kgrc,ckd->kgrd', weights.astype(jnp.bfloat16), value_heads, p...  12.5 us
    gather x2, local copies, waits for them, and re-layouts, one_step(): key_doc = jnp.take(doc_global, key_pos)  12.3 us
    all_gather x1, blocking collectives, local(): value_piece = lax.all_gather(value_block, 'kv', axis=0, tiled=True)  10.7 us
    reduce_sum x2, other arithmetic, block_terms(): row_total = jnp.sum(weights, axis=-1)  8.05 us
    all_to_all x1, starting transfers between devices, local(): lax.all_to_all(key_send, 'head', split_axis=1, concat_axis=0, tiled=True)  6.35 us
    dot_general x2, matrix products, block_terms(): jnp.einsum('rkgd,ckd->kgrc', query_group, key_heads, preferred_element_ty...  5.86 us
  transfers between devices with their start and end apart: 6, of which 2 were waited for; matrix products, arithmetic and copies ran while one was open for 6% of the time, Pallas kernels for 0%

profile of v1, /device:TPU:0, one launch (start us, length us, event | category | flops | bytes accessed | tf_op | source)
XLA Modules:
  0.0 169.8 jit_solution(11300037326310674453)
XLA Ops:
  0.0 0.0 copy-start
  0.0 0.9 copy-done
  0.9 0.7 copy_bitcast_fusion.2
  1.6 6.4 %all-to-all-start = ((bf16[64,8,128]{2,0,1:T(8,128)(2,1)}), bf16[64,8,128]{2,0,1:T(8,128)(2,1)S(1)}, u32[]{:S(2)}, u32[]{:S(2)}) async-start(bf16[64,8,128]{2,0,1:T(8,128)(2,1)} %copy_bitcast_fusion.2), calls=%async_computation | async-start | bytes 262144 | tf_op jit(solution)/shard_map/all_to_all | solution.py:76
  7.9 1.6 copy_bitcast_fusion.1
  9.5 5.2 %all-to-all-done = bf16[64,8,128]{2,0,1:T(8,128)(2,1)S(1)} async-done(((bf16[64,8,128]{2,0,1:T(8,128)(2,1)}), bf16[64,8,128]{2,0,1:T(8,128)(2,1)S(1)}, u32[]{:S(2)}, u32[]{:S(2)}) %all-to-all-start) | async-done | bytes 131104 | tf_op jit(solution)/shard_map/all_to_all | solution.py:76
  14.7 3.4 %all-to-all-start.2 = ((bf16[64,8,128]{2,0,1:T(8,128)(2,1)}), bf16[64,8,128]{2,0,1:T(8,128)(2,1)S(1)}, u32[]{:S(2)}, u32[]{:S(2)}) async-start(bf16[64,8,128]{2,0,1:T(8,128)(2,1)} %copy_bitcast_fusion.1), calls=%async_computation.2 | async-start | bytes 262144 | tf_op jit(solution)/shard_map/all_to_all | solution.py:77
  18.1 1.5 collective-permute-start
  19.6 2.3 %copy.30 = bf16[8,8,8,1024]{3,2,0,1:T(8,128)(2,1)} copy(bf16[8,8,8,1024]{3,2,1,0:T(8,128)(2,1)} %bitcast.124) | data formatting | bytes 2097152 | tf_op jit(solution)/shard_map/all_to_all | solution.py:75
  21.9 2.9 %all-to-all-done.2 = bf16[64,8,128]{2,0,1:T(8,128)(2,1)S(1)} async-done(((bf16[64,8,128]{2,0,1:T(8,128)(2,1)}), bf16[64,8,128]{2,0,1:T(8,128)(2,1)S(1)}, u32[]{:S(2)}, u32[]{:S(2)}) %all-to-all-start.2) | async-done | bytes 131104 | tf_op jit(solution)/shard_map/all_to_all | solution.py:77
  24.8 3.6 %all-to-all-start.1 = ((bf16[64,8,1024]{2,0,1:T(8,128)(2,1)}), bf16[64,8,1024]{2,0,1:T(8,128)(2,1)S(1)}, u32[]{:S(2)}, u32[]{:S(2)}) async-start(bf16[64,8,1024]{2,0,1:T(8,128)(2,1)} %bitcast.93), calls=%async_computation.1 | async-start | bytes 2097152 | tf_op jit(solution)/shard_map/all_to_all | solution.py:75
  28.3 0.0 collective-permute-done
  28.3 1.5 collective-permute-start.1
  29.9 1.3 dynamic-slice
  31.9 0.9 dynamic-update-slice
  32.8 42.4 %all-reduce = s32[2048]{0:T(1024)S(1)} all-reduce(s32[2048]{0:T(1024)S(1)} %dynamic-update-slice), channel_id=1, replica_groups=mesh['head'=8,'kv'=4] {'kv','head'}, use_global_device_ids=true, to_apply=%add | all-reduce | flops 2048 | bytes 16384
  75.1 3.1 %gather_fusion.1 = s32[512]{0:T(512)S(1)} fusion(s32[2048]{0:T(1024)S(1)} %all-reduce, s32[1024]{0:T(1024)S(1)} %pad_clamp_fusion), kind=kCustom, calls=%fused_computation.1 | custom fusion | bytes 6144 | tf_op jit(solution)/shard_map/jit(_take)/gather | solution.py:87
  78.3 0.0 collective-permute-done.1
  78.3 2.3 %collective-permute-start.2 = (bf16[512,128]{1,0:T(8,128)(2,1)S(1)}, bf16[512,128]{1,0:T(8,128)(2,1)S(1)}, u32[]{:S(2)}, u32[]{:S(2)}) collective-permute-start(bf16[512,128]{1,0:T(8,128)(2,1)S(1)} %collective-permute-done.1), channel_id=1, source_target_pairs={{0,1},{1,2},{2,3},{3,0},{4,5},{5,6},{6,7},{7,4},{8,9},{9,10},{10,1... | collective-permute-start | bytes 393224 | tf_op jit(solution)/shard_map/ppermute | solution.py:17
  80.6 10.7 %all_gather.7 = bf16[2048,128]{1,0:T(8,128)(2,1)S(1)} all-gather(bf16[512,128]{1,0:T(8,128)(2,1)S(1)} %bitcast.126), channel_id=1, replica_groups=mesh['head'=8,'kv'=4] {'kv'}, dimensions={0}, use_global_device_ids=true | all-gather | bytes 655360 | tf_op jit(solution)/shard_map/all_gather | solution.py:96
  91.3 0.0 collective-permute-done.2
  91.6 0.0 all-to-all-done.1
  91.6 0.3 copy.26
  91.9 0.1 copy.18
  92.0 43.6 %while.18 = (s32[]{:T(128)}, f32[1,8,512]{2,1,0:T(8,128)S(1)}, f32[1,8,512]{2,1,0:T(8,128)S(1)}, f32[1,8,512,128]{3,2,1,0:T(8,128)}, s32[2048]{0:T(1024)S(1)}, /...) while((s32[]{:T(128)}, f32[1,8,512]{2,1,0:T(8,128)S(1)}, ...), condition=%wide.region_3.4_spmd.clone, body=%wide.region_0.3_spmd.clone.sunk | while | flops 2205726208 | bytes 75335952 | solution.py:111
  92.3 6.2 %gather_fusion = s32[1024]{0:T(1024)S(1)} fusion(s32[2048]{0:T(1024)S(1)} %get-tuple-element.370, s32[1024]{0:T(1024)S(1)} %broadcast_clamp_fusion.2), kind=kCustom, calls=%fused_computation.clone.clone.1 | custom fusion | bytes 12288 | tf_op jit(solution)/shard_map/while/body/eval_jaxpr/jit(_take)/gather | solution.py:105
  98.5 0.8 compare_and_fusion.2
  99.3 2.9 %fusion.41 = (f32[8,512]{1,0:T(8,128)S(1)}, f32[1024,512,8]{1,0,2:T(8,128)S(1)}) fusion(pred[512,1024]{0,1:T(8,128)(4,1)S(1)} %compare_and_fusion.2, bf16[512,1,8,128]{3,0,2,1:T(8,128)(2,1)S(1)} %get-tuple-element.373, bf16[2048,128]{1,0:T(8,128)(2,1)S(1)} %get-tuple-element.372, s32[]{:T(128)S(6)} %select_n.160), kind=kOutput, calls=%fused_computation.5.clone.1 | convolution fusion | flops 1086320640 | bytes 18628612 | tf_op jit(solution)/shard_map/while/body/eval_jaxpr/rkgd,ckd->kgrc/dot_general | solution.py:37
  102.2 0.0 copy-start.1
  102.3 4.0 %fusion.43 = f32[8,512]{1,0:T(8,128)S(1)} fusion(f32[1024,512,8]{1,0,2:T(8,128)S(1)} %get-tuple-element.334, f32[8,512]{1,0:T(8,128)S(1)} %get-tuple-element.332, pred[512,1024]{0,1:T(8,128)(4,1)S(1)} %compare_and_fusion.2), kind=kLoop, calls=%fused_computation.7.clone.1 | loop fusion | flops 20967424 | bytes 17334272 | tf_op jit(solution)/shard_map/while/body/eval_jaxpr/reduce_sum | solution.py:44
  106.3 0.0 copy-done.1
  106.4 6.2 %bitcast_add_fusion.2 = f32[1,8,512,128]{3,2,1,0:T(8,128)S(1)} fusion(f32[1,8,512,128]{3,2,1,0:T(8,128)S(1)} %copy-done.1, f32[1024,512,8]{1,0,2:T(8,128)S(1)} %get-tuple-element.334, f32[8,512]{1,0:T(8,128)S(1)} %get-tuple-element.332, pred[512,1024]{0,1:T(8,128)(4,1)S(1)} %compare_and_fusion.2, f32[8,512]{1,0:T(8,128)S(1)} %get-tuple-element.336, ...), kind=kOutput, calls=%fused_computation.11.clone.1 | convolution fusion | flops 1096810496 | bytes 21807108 | tf_op jit(solution)/shard_map/while/body/eval_jaxpr/kgrc,ckd->kgrd/dot_general | solution.py:45
  112.6 0.0 copy-start.2
  112.6 1.3 copy-done.2
  114.0 6.2 %gather_fusion = s32[1024]{0:T(1024)S(1)} fusion(s32[2048]{0:T(1024)S(1)} %get-tuple-element.370, s32[1024]{0:T(1024)S(1)} %broadcast_clamp_fusion.2), kind=kCustom, calls=%fused_computation.clone.clone.1 | custom fusion | bytes 12288 | tf_op jit(solution)/shard_map/while/body/eval_jaxpr/jit(_take)/gather | solution.py:105
  120.2 0.8 compare_and_fusion.2
  121.0 2.9 %fusion.41 = (f32[8,512]{1,0:T(8,128)S(1)}, f32[1024,512,8]{1,0,2:T(8,128)S(1)}) fusion(pred[512,1024]{0,1:T(8,128)(4,1)S(1)} %compare_and_fusion.2, bf16[512,1,8,128]{3,0,2,1:T(8,128)(2,1)S(1)} %get-tuple-element.373, bf16[2048,128]{1,0:T(8,128)(2,1)S(1)} %get-tuple-element.372, s32[]{:T(128)S(6)} %select_n.160), kind=kOutput, calls=%fused_computation.5.clone.1 | convolution fusion | flops 1086320640 | bytes 18628612 | tf_op jit(solution)/shard_map/while/body/eval_jaxpr/rkgd,ckd->kgrc/dot_general | solution.py:37
  124.0 0.0 copy-start.1
  124.0 4.0 %fusion.43 = f32[8,512]{1,0:T(8,128)S(1)} fusion(f32[1024,512,8]{1,0,2:T(8,128)S(1)} %get-tuple-element.334, f32[8,512]{1,0:T(8,128)S(1)} %get-tuple-element.332, pred[512,1024]{0,1:T(8,128)(4,1)S(1)} %compare_and_fusion.2), kind=kLoop, calls=%fused_computation.7.clone.1 | loop fusion | flops 20967424 | bytes 17334272 | tf_op jit(solution)/shard_map/while/body/eval_jaxpr/reduce_sum | solution.py:44
  128.1 0.0 copy-done.1
  128.1 6.2 %bitcast_add_fusion.2 = f32[1,8,512,128]{3,2,1,0:T(8,128)S(1)} fusion(f32[1,8,512,128]{3,2,1,0:T(8,128)S(1)} %copy-done.1, f32[1024,512,8]{1,0,2:T(8,128)S(1)} %get-tuple-element.334, f32[8,512]{1,0:T(8,128)S(1)} %get-tuple-element.332, pred[512,1024]{0,1:T(8,128)(4,1)S(1)} %compare_and_fusion.2, f32[8,512]{1,0:T(8,128)S(1)} %get-tuple-element.336, ...), kind=kOutput, calls=%fused_computation.11.clone.1 | convolution fusion | flops 1096810496 | bytes 21807108 | tf_op jit(solution)/shard_map/while/body/eval_jaxpr/kgrc,ckd->kgrd/dot_general | solution.py:45
  134.3 0.0 copy-start.2
  134.3 1.3 copy-done.2
  135.7 2.0 %fusion.26 = bf16[512,1,8,128]{3,0,2,1:T(8,128)(2,1)S(1)} fusion(f32[1,8,512,128]{3,2,1,0:T(8,128)} %get-tuple-element.175, f32[8,512]{1,0:T(8,128)S(1)} %bitcast.125), kind=kLoop, calls=%fused_computation.42 | loop fusion | flops 1048576 | bytes 3162112 | tf_op jit(solution)/shard_map/convert_element_type | solution.py:115
  137.6 0.7 copy.19
  138.3 0.5 convert_element_type.19
  138.8 30.0 %all_to_all.70 = bf16[8,64,1024]{2,1,0:T(8,128)(2,1)S(1)} all-to-all(bf16[8,64,1024]{2,1,0:T(8,128)(2,1)S(1)} %convert_element_type.19), channel_id=1, replica_groups=mesh['head'=8,'kv'=4] {'head'}, dimensions={0} | all-to-all | bytes 2097152 | tf_op jit(solution)/shard_map/all_to_all | solution.py:116
  168.8 1.1 copy.25
  (30 shorter events, 0.3 us)
Async XLA Ops:
  0.0 0.9 copy-start
  1.6 13.1 %all-to-all-start = ((bf16[64,8,128]{2,0,1:T(8,128)(2,1)}), bf16[64,8,128]{2,0,1:T(8,128)(2,1)S(1)}, u32[]{:S(2)}, u32[]{:S(2)}) async-start(bf16[64,8,128]{2,0,1:T(8,128)(2,1)} %copy_bitcast_fusion.2), calls=%async_computation | async-start | bytes 262144 | tf_op jit(solution)/shard_map/all_to_all | solution.py:76
  14.7 10.1 %all-to-all-start.2 = ((bf16[64,8,128]{2,0,1:T(8,128)(2,1)}), bf16[64,8,128]{2,0,1:T(8,128)(2,1)S(1)}, u32[]{:S(2)}, u32[]{:S(2)}) async-start(bf16[64,8,128]{2,0,1:T(8,128)(2,1)} %copy_bitcast_fusion.1), calls=%async_computation.2 | async-start | bytes 262144 | tf_op jit(solution)/shard_map/all_to_all | solution.py:77
  18.1 10.3 %collective-permute-start = (bf16[512,128]{1,0:T(8,128)(2,1)S(1)}, bf16[512,128]{1,0:T(8,128)(2,1)S(1)}, u32[]{:S(2)}, u32[]{:S(2)}) collective-permute-start(bf16[512,128]{1,0:T(8,128)(2,1)S(1)} %bitcast.121), channel_id=1, source_target_pairs={{0,1},{1,2},{2,3},{3,0},{4,5},{5,6},{6,7},{7,4},{8,9},{9,10},{10,1... | collective-permute-start | bytes 393224 | tf_op jit(solution)/shard_map/ppermute | solution.py:17
  24.8 66.9 %all-to-all-start.1 = ((bf16[64,8,1024]{2,0,1:T(8,128)(2,1)}), bf16[64,8,1024]{2,0,1:T(8,128)(2,1)S(1)}, u32[]{:S(2)}, u32[]{:S(2)}) async-start(bf16[64,8,1024]{2,0,1:T(8,128)(2,1)} %bitcast.93), calls=%async_computation.1 | async-start | bytes 2097152 | tf_op jit(solution)/shard_map/all_to_all | solution.py:75
  28.3 49.9 %collective-permute-start.1 = (bf16[512,128]{1,0:T(8,128)(2,1)S(1)}, bf16[512,128]{1,0:T(8,128)(2,1)S(1)}, u32[]{:S(2)}, u32[]{:S(2)}) collective-permute-start(bf16[512,128]{1,0:T(8,128)(2,1)S(1)} %collective-permute-done), channel_id=1, source_target_pairs={{0,1},{1,2},{2,3},{3,0},{4,5},{5,6},{6,7},{7,4},{8,9},{9,10},{10,1... | collective-permute-start | bytes 393224 | tf_op jit(solution)/shard_map/ppermute | solution.py:17
  78.3 13.1 %collective-permute-start.2 = (bf16[512,128]{1,0:T(8,128)(2,1)S(1)}, bf16[512,128]{1,0:T(8,128)(2,1)S(1)}, u32[]{:S(2)}, u32[]{:S(2)}) collective-permute-start(bf16[512,128]{1,0:T(8,128)(2,1)S(1)} %collective-permute-done.1), channel_id=1, source_target_pairs={{0,1},{1,2},{2,3},{3,0},{4,5},{5,6},{6,7},{7,4},{8,9},{9,10},{10,1... | collective-permute-start | bytes 393224 | tf_op jit(solution)/shard_map/ppermute | solution.py:17
  102.2 4.1 %copy-start.1 = (f32[1,8,512,128]{3,2,1,0:T(8,128)S(1)}, f32[1,8,512,128]{3,2,1,0:T(8,128)}, u32[]{:S(2)}) copy-start(f32[1,8,512,128]{3,2,1,0:T(8,128)} %get-tuple-element.355) | copy-start | bytes 6291460 | tf_op jit(solution)/shard_map/while
  112.6 1.3 copy-start.2
  124.0 4.1 %copy-start.1 = (f32[1,8,512,128]{3,2,1,0:T(8,128)S(1)}, f32[1,8,512,128]{3,2,1,0:T(8,128)}, u32[]{:S(2)}) copy-start(f32[1,8,512,128]{3,2,1,0:T(8,128)} %get-tuple-element.355) | copy-start | bytes 6291460 | tf_op jit(solution)/shard_map/while
  134.3 1.3 copy-start.2
